TPU v7x, 256 devices: a whole 4x4x8 slice. The times are simulated.
256 devices in a mesh: depth: 64 (over y, z, core), lat: 4 (over x).
Axes of the slice: x: 4, y: 4, z: 8, core: 2. Of those that a mesh axis runs over, the one named last changes fastest.
Arguments:
- sources: float32 [64, 2, 64, 4096], P('depth', None, None, 'lat'), may hold values from -6 to 6
- down_expand: float32 [64, 2, 64, 4096], P('depth', None, None, 'lat'), may hold values from -0.75 to 0.75
- down_project: float32 [64, 2, 64, 4096], P('depth', None, None, 'lat'), may hold values from -0.09375 to 0.09375
- up_expand: float32 [64, 2, 64, 4096], P('depth', None, None, 'lat'), may hold values from -0.75 to 0.75
- up_project: float32 [64, 2, 64, 4096], P('depth', None, None, 'lat'), may hold values from -0.09375 to 0.09375
- down_decay: float32 [64, 64], P('depth'), may hold values from 0.3 to 0.8
- up_decay: float32 [64, 64], P('depth'), may hold values from 0.3 to 0.8
- active_list: int32 [64, 64], P('depth'), may hold values from 0 to 63, each once within a row
- active_count: int32 [64], P('depth'), may hold values from 1 to 64
- incident_down: float32 [2, 64, 4096], P(None, None, 'lat'), may hold values from -6 to 6
- incident_up: float32 [2, 64, 4096], P(None, None, 'lat'), may hold values from -6 to 6
Outputs:
- field: float32 [64, 2, 64, 4096], P('depth', None, None, 'lat')
Inputs may be any that keep to these rules, and one draw needn't show every extreme that they name: Each row of active_list holds every source number once.
All inputs are finite; a program needn't handle non-finite values.
Results may differ from a plain program's by a relative error of at most 0.0003.
Values sent between devices are 32-bit elements; how exact they have to be, the bound alone decides.
A program may use at most 64 MiB of HBM per device.

v0:
```python
import jax
import jax.numpy as jnp
from jax import lax
from jax.sharding import Mesh
from jax.sharding import PartitionSpec as P

DEPTH = ("depth_0", "depth_1", "depth_2")


def passed_along(value, axis, steps):
    count = lax.axis_size(axis)
    first, last = (max(0, -steps), min(count, count - steps))
    return lax.ppermute(value, axis, [(source, source + steps) for source in range(first, last)])


def copy_for_each(value, axis):
    copies = jnp.broadcast_to(value, (lax.axis_size(axis), *value.shape))
    return lax.all_to_all(copies, axis, split_axis=0, concat_axis=0, tiled=True)


def over_copies(value, axis):
    return copy_for_each(value, axis).sum(axis=0)


def packed_total(arrays, axis):
    flat, at, finished = (jnp.concatenate([a.reshape(-1) for a in arrays]), 0, [])
    subtotal = over_copies(flat, axis)
    for a in arrays:
        finished.append(subtotal[at : at + a.size].reshape(a.shape))
        at += a.size
    return tuple(finished)


def nothing_yet(value, identity):
    return jax.tree.map(
        lambda part, zero: jnp.zeros_like(part) + jnp.asarray(zero, part.dtype), value, identity
    )


def gathered_once(value, axis):
    leaves = jax.tree.leaves(value)
    turns = sorted(range(len(leaves)), key=lambda k: -leaves[k].size)
    width = (1, *leaves[turns[0]].shape)[-1]
    lines = [
        jnp.pad(leaves[k].reshape(-1), (0, -leaves[k].size % width)).reshape(-1, width)
        for k in turns
    ]
    both, at, found = (lax.all_gather(jnp.concatenate(lines), axis), 0, {})
    for k, line in zip(turns, lines):
        share = both[:, at : at + len(line)].reshape(len(both), -1)
        found[k] = share[:, : leaves[k].size].reshape(-1, *leaves[k].shape)
        at += len(line)
    numbers = iter(range(len(leaves)))
    return jax.tree.map(lambda _: found[next(numbers)], value)


def prefix_by_axis(value, axes, combine, identity, reverse):
    before = start = nothing_yet(value, identity)
    subtotal = value
    for axis in reversed(axes):
        peers, place = (lax.axis_size(axis), lax.axis_index(axis))
        pieces = gathered_once(subtotal, axis)
        inside, subtotal = (start, start)
        for k in reversed(range(peers)) if reverse else range(peers):
            passed = k > place if reverse else k < place
            subtotal = combine(subtotal, jax.tree.map(lambda part: part[k], pieces))
            inside = jax.tree.map(lambda new, old: jnp.where(passed, new, old), subtotal, inside)
        before = combine(inside, before)
    return before


def contract(left, right):
    hp = lax.Precision.HIGHEST
    dims = (((1,), (1,)), ((), ()))

    def prod(a, b):
        return lax.dot_general(a, b, dims, precision=hp, preferred_element_type=jnp.float32)

    real = prod(left[0], right[0]) - prod(left[1], right[1])
    imag = prod(left[0], right[1]) + prod(left[1], right[0])
    return jnp.stack([real, imag])


def expand(coef, basis):
    hp = lax.Precision.HIGHEST
    dims = (((0,), (0,)), ((), ()))

    def prod(a, b):
        return lax.dot_general(a, b, dims, precision=hp, preferred_element_type=jnp.float32)

    real = prod(coef[0], basis[0]) - prod(coef[1], basis[1])
    imag = prod(coef[0], basis[1]) + prod(coef[1], basis[0])
    return jnp.stack([real, imag])


def cmatmul(first, second):
    hp = lax.Precision.HIGHEST

    def prod(a, b):
        return jnp.dot(a, b, precision=hp, preferred_element_type=jnp.float32)

    real = prod(first[0], second[0]) - prod(first[1], second[1])
    imag = prod(first[0], second[1]) + prod(first[1], second[0])
    return jnp.stack([real, imag])


def compose(earlier, later):
    return (cmatmul(later[0], earlier[0]), cmatmul(later[0], earlier[1]) + later[1])


def body(
    sources,
    down_expand,
    down_project,
    up_expand,
    up_project,
    down_decay,
    up_decay,
    active_list,
    active_count,
    incident_down,
    incident_up,
):
    nsrc = sources.shape[2]
    nrank = down_expand.shape[2]
    places = jnp.arange(nsrc, dtype=jnp.int32)
    valid = (places < active_count[0]).astype(jnp.float32)
    hits = (active_list[0][:, None] == places[None, :]).astype(jnp.float32)
    mask = jnp.sum(valid[:, None] * hits, axis=0)
    local = sources[0] * mask[None, :, None]
    own_group = lax.axis_index(DEPTH)
    at_top = own_group == 0
    at_bottom = own_group == lax.axis_size(DEPTH) - 1
    prev_wave, prev_basis = passed_along((local, down_expand[0]), DEPTH, 1)
    next_wave, next_basis = passed_along((local, up_expand[0]), DEPTH, -1)
    prev_wave = jnp.where(at_top, incident_down, prev_wave)
    next_wave = jnp.where(at_bottom, incident_up, next_wave)
    parts = (
        contract(down_project[0], prev_wave),
        contract(down_project[0], prev_basis),
        contract(up_project[0], next_wave),
        contract(up_project[0], next_basis),
    )
    down_offset, down_map, up_offset, up_map = packed_total(
        (parts[0], parts[1], parts[2], parts[3]), "lat"
    )
    down_scale = down_decay[0][None, :, None]
    up_scale = up_decay[0][None, :, None]
    down_offset = down_scale * down_offset
    down_map = down_scale * down_map
    up_offset = up_scale * up_offset
    up_map = up_scale * up_map
    unit = jnp.stack([jnp.eye(nrank, dtype=jnp.float32), jnp.zeros((nrank, nrank), jnp.float32)])
    identity = (unit, jnp.zeros((2, nrank, nsrc), jnp.float32))
    _, down_prior = prefix_by_axis((down_map, down_offset), DEPTH, compose, identity, False)
    _, up_prior = prefix_by_axis((up_map, up_offset), DEPTH, compose, identity, True)
    down_coef = down_offset + cmatmul(down_map, down_prior)
    up_coef = up_offset + cmatmul(up_map, up_prior)
    field = local + expand(down_coef, down_expand[0]) + expand(up_coef, up_expand[0])
    return field[None]


def solution(mesh):
    split = Mesh(
        mesh.devices.reshape(4, 8, 2, mesh.shape["lat"]), ("depth_0", "depth_1", "depth_2", "lat")
    )
    placed = (
        P(DEPTH, None, None, "lat"),
        P(DEPTH, None, None, "lat"),
        P(DEPTH, None, None, "lat"),
        P(DEPTH, None, None, "lat"),
        P(DEPTH, None, None, "lat"),
        P(DEPTH, None),
        P(DEPTH, None),
        P(DEPTH, None),
        P(DEPTH),
        P(None, None, "lat"),
        P(None, None, "lat"),
    )
    return jax.shard_map(
        body, mesh=split, in_specs=placed, out_specs=P(DEPTH, None, None, "lat"), check_vma=False
    )
```

profile of v0, /device:TPU:8, one launch (start us, length us, event | category | flops | bytes accessed | tf_op | source)
XLA Modules:
  0.0 192.3 jit_solution(15308575957363059932)
XLA Ops:
  1.4 2.0 %bitcast_multiply_fusion = f32[2,64,1024]{2,1,0:T(8,128)} fusion(f32[1,2,64,1024]{3,2,1,0:T(8,128)} %param.11, f32[64]{0:T(128)S(1)} %select_reduce_fusion), kind=kLoop, calls=%fused_computation.202 | loop fusion | flops 131072 | bytes 1048832 | tf_op jit(solution)/shard_map/mul | solution.py:130
  3.5 1.9 collective-permute-start
  5.4 7.1 %collective-permute-start.2 = (f32[2,64,1024]{2,1,0:T(8,128)}, f32[2,64,1024]{2,1,0:T(8,128)}, u32[]{:S(2)}, u32[]{:S(2)}) collective-permute-start(f32[2,64,1024]{2,1,0:T(8,128)} %bitcast_multiply_fusion), channel_id=1, source_target_pairs={{4,0},{8,4},{12,8},{16,12},{20,16},{24,20},{28,24},{32,28},{36,32}... | collective-permute-start | bytes 1572872 | tf_op jit(solution)/shard_map/ppermute | solution.py:13
  12.5 1.9 collective-permute-start.1
  14.4 5.8 %collective-permute-start.3 = (f32[2,64,1024]{2,1,0:T(8,128)S(1)}, f32[2,64,1024]{2,1,0:T(8,128)S(1)}, u32[]{:S(2)}, u32[]{:S(2)}) collective-permute-start(f32[2,64,1024]{2,1,0:T(8,128)S(1)} %bitcast.1237), channel_id=1, source_target_pairs={{4,0},{8,4},{12,8},{16,12},{20,16},{24,20},{28,24},{32,28},{36,32}... | collective-permute-start | bytes 1572872 | tf_op jit(solution)/shard_map/ppermute | solution.py:13
  20.3 0.9 copy-done.2
  23.0 1.1 broadcast_select_fusion
  29.1 1.1 broadcast_in_dim.4
  30.2 4.3 %all-to-all-start = ((f32[4,1,32768]{2,1,0:T(1,128)}), f32[4,1,32768]{2,1,0:T(1,128)S(1)}, u32[]{:S(2)}, u32[]{:S(2)}) async-start(f32[4,1,32768]{2,1,0:T(1,128)} %broadcast_in_dim.4), calls=%async_computation | async-start | bytes 1048576 | tf_op jit(solution)/shard_map/all_to_all | solution.py:18
  36.0 6.6 %all-to-all-done = f32[4,1,32768]{2,1,0:T(1,128)S(1)} async-done(((f32[4,1,32768]{2,1,0:T(1,128)}), f32[4,1,32768]{2,1,0:T(1,128)S(1)}, u32[]{:S(2)}, u32[]{:S(2)}) %all-to-all-start) | async-done | bytes 524320 | tf_op jit(solution)/shard_map/all_to_all | solution.py:18
  43.3 2.0 %all-gather.3 = f32[512,64]{1,0:T(8,128)S(1)} all-gather(f32[256,64]{1,0:T(8,128)S(1)} %pad_maximum_fusion.4), channel_id=5, replica_groups=mesh['depth_0'=4,'depth_1'=8,'depth_2'=2,'lat'=4] {'depth_2'}, dimensions={0}, use_global_device_ids=true | all-gather | bytes 196608 | tf_op jit(solution)/shard_map/all_gather | solution.py:48
  47.8 27.3 %all-gather.4 = f32[2048,64]{1,0:T(8,128)S(1)} all-gather(f32[256,64]{1,0:T(8,128)S(1)} %pad_maximum_fusion.5), channel_id=6, replica_groups=mesh['depth_0'=4,'depth_1'=8,'depth_2'=2,'lat'=4] {'depth_1'}, dimensions={0}, use_global_device_ids=true | all-gather | bytes 589824 | tf_op jit(solution)/shard_map/all_gather | solution.py:48
  77.9 0.9 fusion.31
  78.9 0.9 fusion.30
  81.7 0.9 fusion.29
  82.6 0.9 fusion.28
  85.4 0.9 fusion.27
  89.1 1.0 fusion.25
  90.2 0.9 fusion.24
  106.8 13.1 %all-gather.5 = f32[1024,64]{1,0:T(8,128)S(1)} all-gather(f32[256,64]{1,0:T(8,128)S(1)} %pad_maximum_fusion.6), channel_id=7, replica_groups=mesh['depth_0'=4,'depth_1'=8,'depth_2'=2,'lat'=4] {'depth_0'}, dimensions={0}, use_global_device_ids=true | all-gather | bytes 327680 | tf_op jit(solution)/shard_map/all_gather | solution.py:48
  126.8 2.0 %all-gather = f32[512,64]{1,0:T(8,128)S(1)} all-gather(f32[256,64]{1,0:T(8,128)S(1)} %pad_maximum_fusion.1), channel_id=2, replica_groups=mesh['depth_0'=4,'depth_1'=8,'depth_2'=2,'lat'=4] {'depth_2'}, dimensions={0}, use_global_device_ids=true | all-gather | bytes 196608 | tf_op jit(solution)/shard_map/all_gather | solution.py:48
  131.2 26.9 %all-gather.1 = f32[2048,64]{1,0:T(8,128)S(1)} all-gather(f32[256,64]{1,0:T(8,128)S(1)} %pad_maximum_fusion.2), channel_id=3, replica_groups=mesh['depth_0'=4,'depth_1'=8,'depth_2'=2,'lat'=4] {'depth_1'}, dimensions={0}, use_global_device_ids=true | all-gather | bytes 589824 | tf_op jit(solution)/shard_map/all_gather | solution.py:48
  169.4 13.0 %all-gather.2 = f32[1024,64]{1,0:T(8,128)S(1)} all-gather(f32[256,64]{1,0:T(8,128)S(1)} %pad_maximum_fusion.3), channel_id=4, replica_groups=mesh['depth_0'=4,'depth_1'=8,'depth_2'=2,'lat'=4] {'depth_0'}, dimensions={0}, use_global_device_ids=true | all-gather | bytes 327680 | tf_op jit(solution)/shard_map/all_gather | solution.py:48
  191.4 0.9 fusion.80
  (353 shorter events, 64.6 us)
Async XLA Ops:
  0.7 0.7 copy-start.10
  1.4 11.1 %copy-start.5 = (f32[1,2,64,1024]{3,2,1,0:T(8,128)S(1)}, f32[1,2,64,1024]{3,2,1,0:T(8,128)}, u32[]{:S(2)}) copy-start(f32[1,2,64,1024]{3,2,1,0:T(8,128)} %param.12) | copy-start | bytes 1572868
  1.4 13.0 %copy-start.4 = (f32[1,2,64,1024]{3,2,1,0:T(8,128)S(1)}, f32[1,2,64,1024]{3,2,1,0:T(8,128)}, u32[]{:S(2)}) copy-start(f32[1,2,64,1024]{3,2,1,0:T(8,128)} %param.14) | copy-start | bytes 1572868
  3.5 16.8 %collective-permute-start = (f32[2,64,1024]{2,1,0:T(8,128)}, f32[2,64,1024]{2,1,0:T(8,128)S(1)}, u32[]{:S(2)}, u32[]{:S(2)}) collective-permute-start(f32[2,64,1024]{2,1,0:T(8,128)} %bitcast_multiply_fusion), channel_id=1, source_target_pairs={{0,4},{4,8},{8,12},{12,16},{16,20},{20,24},{24,28},{28,32},{32,36}... | collective-permute-start | bytes 1572872 | tf_op jit(solution)/shard_map/ppermute | solution.py:13
  5.4 17.4 %collective-permute-start.2 = (f32[2,64,1024]{2,1,0:T(8,128)}, f32[2,64,1024]{2,1,0:T(8,128)}, u32[]{:S(2)}, u32[]{:S(2)}) collective-permute-start(f32[2,64,1024]{2,1,0:T(8,128)} %bitcast_multiply_fusion), channel_id=1, source_target_pairs={{4,0},{8,4},{12,8},{16,12},{20,16},{24,20},{28,24},{32,28},{36,32}... | collective-permute-start | bytes 1572872 | tf_op jit(solution)/shard_map/ppermute | solution.py:13
  12.5 13.1 %collective-permute-start.1 = (f32[2,64,1024]{2,1,0:T(8,128)S(1)}, f32[2,64,1024]{2,1,0:T(8,128)S(1)}, u32[]{:S(2)}, u32[]{:S(2)}) collective-permute-start(f32[2,64,1024]{2,1,0:T(8,128)S(1)} %bitcast.1238), channel_id=1, source_target_pairs={{0,4},{4,8},{8,12},{12,16},{16,20},{20,24},{24,28},{28,32},{32,36}... | collective-permute-start | bytes 1572872 | tf_op jit(solution)/shard_map/ppermute | solution.py:13
  14.4 13.1 %collective-permute-start.3 = (f32[2,64,1024]{2,1,0:T(8,128)S(1)}, f32[2,64,1024]{2,1,0:T(8,128)S(1)}, u32[]{:S(2)}, u32[]{:S(2)}) collective-permute-start(f32[2,64,1024]{2,1,0:T(8,128)S(1)} %bitcast.1237), channel_id=1, source_target_pairs={{4,0},{8,4},{12,8},{16,12},{20,16},{24,20},{28,24},{32,28},{36,32}... | collective-permute-start | bytes 1572872 | tf_op jit(solution)/shard_map/ppermute | solution.py:13
  20.2 1.0 copy-start.2
  22.0 1.0 copy-start.7
  22.7 1.4 copy-start.3
  30.2 12.4 %all-to-all-start = ((f32[4,1,32768]{2,1,0:T(1,128)}), f32[4,1,32768]{2,1,0:T(1,128)S(1)}, u32[]{:S(2)}, u32[]{:S(2)}) async-start(f32[4,1,32768]{2,1,0:T(1,128)} %broadcast_in_dim.4), calls=%async_computation | async-start | bytes 1048576 | tf_op jit(solution)/shard_map/all_to_all | solution.py:18
  34.5 0.7 copy-start.8
  35.2 0.7 copy-start.9
  75.1 1.0 copy-start
  89.1 11.6 %copy-start.1 = (f32[2048,64]{1,0:T(8,128)S(1)}, f32[2048,64]{1,0:T(8,128)}, u32[]{:S(2)}) copy-start(f32[2048,64]{1,0:T(8,128)} %copy-done) | copy-start | bytes 1572868
  190.3 1.0 copy-start.6
where the time goes:
time: 194 us; the launch traced here: 192 us
  blocking collectives  84.3 us (43%)
  matrix products  64.1 us (33%)
  starting transfers between devices  21 us (11%)
  local copies, waits for them, and re-layouts  6.88 us (4%)
  waiting for transfers between devices  6.6 us (3%)
  other arithmetic  6.24 us (3%)
  between operations  3.22 us (2%)
    all_gather x6, blocking collectives, gathered_once(): both, at, found = (lax.all_gather(jnp.concatenate(lines), axis), 0, {})  84.3 us
    dot_general x220, matrix products, prod(): return jnp.dot(a, b, precision=hp, preferred_element_type=jnp.float32)  55.1 us
    ppermute x4, starting transfers between devices, passed_along(): lax.ppermute(value, axis, [(source, source + steps) for source in range(f...  16.7 us
    dot_general x24, matrix products, prod(): lax.dot_general(a, b, dims, precision=hp, preferred_element_type=jnp.floa...  9.01 us
    all_to_all x1, waiting for transfers between devices, copy_for_each(): return lax.all_to_all(copies, axis, split_axis=0, concat_axis=0, tiled=True)  6.59 us
    unnamed x22, local copies, waits for them, and re-layouts  4.44 us
    all_to_all x1, starting transfers between devices, copy_for_each(): return lax.all_to_all(copies, axis, split_axis=0, concat_axis=0, tiled=True)  4.31 us
  transfers between devices with their start and end apart: 5, of which 1 were waited for; matrix products, arithmetic and copies ran while one was open for 3% of the time, Pallas kernels for 0%

commit v1 on v0

v1 whole, which is shorter than its diff:
```python
import functools

import jax
import jax.numpy as jnp
from jax import lax
from jax.experimental import pallas as pl
from jax.experimental.pallas import tpu as pltpu
from jax.sharding import PartitionSpec as P

F32 = jnp.float32
BF16 = jnp.bfloat16
MESH = pl.DeviceIdType.MESH
CHUNKS = 4


def halves(value):
    high = value.astype(BF16)
    return high, (value - high.astype(F32)).astype(BF16)


def dot(left, right):
    return lax.dot_general(left, right, (((1,), (0,)), ((), ())), preferred_element_type=F32)


def dot_rows(left, right):
    return lax.dot_general(left, right, (((1,), (1,)), ((), ())), preferred_element_type=F32)


def lanes_of(shape):
    return lax.broadcasted_iota(jnp.int32, shape, 1)


def compose(later, earlier):
    n = later.shape[0] // 2
    real, imag = later[:n], later[n:]
    left = lanes_of(real.shape) < n
    top = jnp.where(left, real, -pltpu.roll(imag, n, 1))
    low = jnp.where(left, imag, pltpu.roll(real, n, 1))
    lhs_h, lhs_l = halves(jnp.concatenate([top, low], axis=0))
    rhs_h, rhs_l = halves(earlier)
    out = dot(jnp.concatenate([lhs_h, lhs_l], axis=1), jnp.concatenate([rhs_h, rhs_h], axis=0))
    out = out + dot(lhs_h, rhs_l)
    return out + jnp.where(lanes_of(later.shape) < n, 0.0, later)


def kernel(
    dims,
    src_hbm, dexp_hbm, dproj_hbm, uexp_hbm, uproj_hbm, ddec_ref, udec_ref, list_ref, count_ref, incd_hbm, incu_hbm,
    out_ref,
    src, exps, inc, proj, wh, wl, xsend, xrecv, state, zsend, zrecv, ysend, yrecv, start, qown, qsend, qrecv, tother,
    load_sem, psend_sem, precv_sem, xsend_sem, xrecv_sem, tsend_sem, trecv_sem, zsend_sem, zrecv_sem,
    ysend_sem, yrecv_sem, qsend_sem, qrecv_sem,
):
    ny, nz, nx = dims
    groups = ny * nz * 2
    rounds = nz.bit_length() - 1
    masks = [1 << k for k in range(rounds - 1)] + [nz - 1]
    g = lax.axis_index("depth")
    x = lax.axis_index("lat")
    core = lax.rem(g, 2)
    z = lax.rem(lax.div(g, 2), nz)
    y = lax.div(g, 2 * nz)
    zz = jnp.where(core == 0, z, nz - 1 - z)
    yy = jnp.where(core == 0, y, ny - 1 - y)
    mate = g + 1 - 2 * core
    is_first = g == 0
    is_last = g == groups - 1
    begins = jnp.logical_and(yy == 0, zz == 0)

    def place(to_y, to_z):
        return (to_y * nz + to_z) * 2 + core

    def xor(value, mask):
        out = value
        for bit in range(rounds):
            if mask >> bit & 1:
                set_ = lax.rem(lax.div(value, 1 << bit), 2)
                out = out + (1 << bit) * (1 - 2 * set_)
        return out

    z_peers = [place(y, xor(z, mask)) for mask in masks]
    y_peers = [place(lax.rem(y + o, ny), z) for o in range(1, ny)]

    barrier = pltpu.get_barrier_semaphore()
    for o in range(1, nx):
        pl.semaphore_signal(barrier, inc=1, device_id=(g, lax.rem(x + o, nx)), device_id_type=MESH)
    for peer in z_peers + y_peers:
        pl.semaphore_signal(barrier, inc=1, device_id=(peer, x), device_id_type=MESH)

    @pl.when(jnp.logical_not(is_first))
    def _():
        pl.semaphore_signal(barrier, inc=1, device_id=(g - 1, x), device_id_type=MESH)

    @pl.when(jnp.logical_not(is_last))
    def _():
        pl.semaphore_signal(barrier, inc=1, device_id=(g + 1, x), device_id_type=MESH)

    loads = [
        pltpu.make_async_copy(dexp_hbm, exps.at[0], load_sem.at[0]),
        pltpu.make_async_copy(src_hbm, src, load_sem.at[1]),
        pltpu.make_async_copy(uexp_hbm, exps.at[1], load_sem.at[2]),
    ]
    for copy in loads:
        copy.start()

    inc_copies = [
        pltpu.make_async_copy(incd_hbm, inc, load_sem.at[3]),
        pltpu.make_async_copy(incu_hbm, inc, load_sem.at[3]),
    ]
    pl.when(is_first)(inc_copies[0].start)
    pl.when(is_last)(inc_copies[1].start)

    edge = jnp.where(jnp.logical_or(is_first, is_last), 1, 0)
    pl.semaphore_wait(barrier, nx - 1 + len(z_peers) + len(y_peers) + 2 - edge)

    size = proj.shape[3]
    sends = []
    for k in range(CHUNKS):
        rows = pl.ds(k * size, size)
        down = pltpu.make_async_remote_copy(
            src_ref=dproj_hbm.at[:, rows], dst_ref=proj.at[0, k],
            send_sem=psend_sem.at[0, k], recv_sem=precv_sem.at[0, k],
            device_id=(jnp.maximum(g - 1, 0), x), device_id_type=MESH,
        )
        up = pltpu.make_async_remote_copy(
            src_ref=uproj_hbm.at[:, rows], dst_ref=proj.at[1, k],
            send_sem=psend_sem.at[1, k], recv_sem=precv_sem.at[1, k],
            device_id=(jnp.minimum(g + 1, groups - 1), x), device_id_type=MESH,
        )
        own_down = pltpu.make_async_copy(dproj_hbm.at[:, rows], proj.at[1, k], precv_sem.at[1, k])
        own_up = pltpu.make_async_copy(uproj_hbm.at[:, rows], proj.at[0, k], precv_sem.at[0, k])

        @pl.when(jnp.logical_not(is_first))
        def _():
            down.start()

        @pl.when(is_first)
        def _():
            own_down.start()

        @pl.when(jnp.logical_not(is_last))
        def _():
            up.start()

        @pl.when(is_last)
        def _():
            own_up.start()

        sends.append((down, up))

    n = src.shape[1]
    square = (n, n)
    row_at = lax.broadcasted_iota(jnp.int32, square, 0)
    lane_at = lanes_of(square)
    valid = jnp.logical_and(list_ref[...] == row_at, lane_at < count_ref[0])
    mask = jnp.sum(jnp.where(valid, 1.0, 0.0), axis=1, keepdims=True)
    for slot, (dec_ref, load) in enumerate(((ddec_ref, loads[0]), (udec_ref, loads[2]))):
        decay = jnp.sum(jnp.where(row_at == lane_at, dec_ref[...], 0.0), axis=1, keepdims=True)
        load.wait()
        for part in range(2):
            high, low = halves(exps[slot, part] * decay)
            wh[slot, pl.ds(2 * part * n, n)] = high
            wl[slot, pl.ds(2 * part * n, n)] = low
    loads[1].wait()
    for part in range(2):
        high, low = halves(src[part] * mask)
        for slot in range(2):
            wh[slot, pl.ds((2 * part + 1) * n, n)] = high
            wl[slot, pl.ds((2 * part + 1) * n, n)] = low
    for slot, at_edge in ((1, is_first), (0, is_last)):

        @pl.when(at_edge)
        def _():
            inc_copies[0].wait()
            for part in range(2):
                high, low = halves(inc[part])
                wh[slot, pl.ds((2 * part + 1) * n, n)] = high
                wl[slot, pl.ds((2 * part + 1) * n, n)] = low

    x_copies = {}
    for k in range(CHUNKS):
        for slot in range(2):
            sends[k][slot].wait_recv()
            p_h, p_l = halves(proj[slot, k].reshape(2 * size, proj.shape[4]))
            both = dot_rows(jnp.concatenate([p_h, p_l], axis=0), wh[slot])
            total = both[: 2 * size] + both[2 * size :] + dot_rows(p_h, wl[slot])
            first, second = total[:size], total[size:]
            xsend[slot, k, 0] = first[:, : 2 * n] - second[:, 2 * n :]
            xsend[slot, k, 1] = first[:, 2 * n :] + second[:, : 2 * n]
            for o in range(1, nx):
                copy = pltpu.make_async_remote_copy(
                    src_ref=xsend.at[slot, k], dst_ref=xrecv.at[slot, k, o - 1],
                    send_sem=xsend_sem.at[slot, k, o - 1], recv_sem=xrecv_sem.at[slot, k, o - 1],
                    device_id=(g, lax.rem(x + o, nx)), device_id_type=MESH,
                )
                copy.start()
                x_copies[slot, k, o] = copy
    for k in range(CHUNKS):
        for slot in range(2):
            total = xsend[slot, k]
            for o in range(1, nx):
                x_copies[slot, k, o].wait_recv()
                total = total + xrecv[slot, k, o - 1]
            for part in range(2):
                state[slot, pl.ds(part * n + k * size, size)] = total[part]

    swap = pltpu.make_async_remote_copy(
        src_ref=state.at[1 - core], dst_ref=tother, send_sem=tsend_sem, recv_sem=trecv_sem,
        device_id=(mate, x), device_id_type=MESH,
    )
    swap.start()
    wide = state.shape[1:]
    in_map = lanes_of(wide) < n
    mine = state[core]
    initial = jnp.where(in_map, 0.0, state[1 - core])
    qown[...] = mine

    @pl.when(begins)
    def _():
        qown[...] = compose(mine, initial)

    swap.wait_recv()
    total = compose(tother[...], qown[...])
    row = lax.broadcasted_iota(jnp.int32, wide, 0)
    prefix = jnp.where(jnp.logical_and(row == lanes_of(wide), in_map), 1.0, 0.0)
    z_copies = []
    for k in range(rounds):
        zsend[k] = total
        copy = pltpu.make_async_remote_copy(
            src_ref=zsend.at[k], dst_ref=zrecv.at[k], send_sem=zsend_sem.at[k], recv_sem=zrecv_sem.at[k],
            device_id=(z_peers[k], x), device_id_type=MESH,
        )
        copy.start()
        z_copies.append(copy)
        copy.wait_recv()
        theirs = zrecv[k]
        after = lax.rem(lax.div(zz, 1 << k), 2) == 1
        if k == 0:
            joined = theirs
        else:
            joined = compose(prefix, theirs)
        prefix = jnp.where(after, joined, prefix)
        total = compose(jnp.where(after, total, theirs), jnp.where(after, theirs, total))

    ysend[...] = total
    y_copies = []
    for o in range(1, ny):
        to_y = jnp.where(core == 0, lax.rem(y + o, ny), lax.rem(y + ny - o, ny))
        copy = pltpu.make_async_remote_copy(
            src_ref=ysend, dst_ref=yrecv.at[o - 1], send_sem=ysend_sem.at[o - 1], recv_sem=yrecv_sem.at[o - 1],
            device_id=(place(to_y, z), x), device_id_type=MESH,
        )
        y_copies.append(copy)
        pl.when(yy + o < ny)(copy.start)

    @pl.when(yy == 0)
    def _():
        qown[...] = jnp.where(begins, initial, prefix)

    for at in range(1, ny):

        @pl.when(yy == at)
        def _():
            for o in range(at, 0, -1):
                y_copies[o - 1].wait_recv()
            here = yrecv[at - 1]
            for o in range(at - 1, 0, -1):
                here = compose(yrecv[o - 1], here)
            qown[...] = compose(prefix, here)

    qsend[...] = compose(mine, qown[...])
    give = pltpu.make_async_remote_copy(
        src_ref=qsend, dst_ref=qrecv, send_sem=qsend_sem, recv_sem=qrecv_sem,
        device_id=(mate, x), device_id_type=MESH,
    )
    give.start()
    give.wait_recv()

    own, other = qown[...], qrecv[...]
    left = lanes_of((n, 2 * n)) < n
    coefs = []
    for value in (jnp.where(core == 0, own, other), jnp.where(core == 0, other, own)):
        turned = jnp.transpose(value)[n:]
        coefs.append(jnp.concatenate([jnp.where(left, turned, -turned), pltpu.roll(turned, n, 1)], axis=0))
    c_h, c_l = halves(jnp.concatenate(coefs, axis=1))
    c_all = jnp.concatenate([c_h, c_l], axis=0)
    width = src.shape[2]
    step = min(256, width)
    for at in range(0, width, step):
        cols = pl.ds(at, step)
        picks = [(slot, pl.ds(2 * part * n, n)) for slot in range(2) for part in range(2)]
        e_h = jnp.concatenate([wh[slot, rows, cols] for slot, rows in picks], axis=0)
        e_l = jnp.concatenate([wl[slot, rows, cols] for slot, rows in picks], axis=0)
        both = dot(c_all, e_h)
        terms = both[: 2 * n] + both[2 * n :] + dot(c_h, e_l)
        for part in range(2):
            out_ref[part, :, cols] = src[part, :, cols] * mask + terms[part * n : (part + 1) * n]

    for k, (down, up) in enumerate(sends):
        pl.when(jnp.logical_not(is_first))(down.wait_send)
        pl.when(jnp.logical_not(is_last))(up.wait_send)
    for copy in x_copies.values():
        copy.wait_send()
    swap.wait_send()
    for copy in z_copies:
        copy.wait_send()
    for o, copy in enumerate(y_copies, 1):
        pl.when(yy + o < ny)(copy.wait_send)
    give.wait_send()


def sweeps(dims, *args):
    sources, dexp, dproj, uexp, uproj, ddec, udec, active, count, incd, incu = args
    ny, nz, nx = dims
    _, _, n, width = sources.shape
    size = n // CHUNKS
    rounds = nz.bit_length() - 1
    full = (2 * n, 2 * n)
    anywhere = pl.BlockSpec(memory_space=pl.ANY)
    vmem = pl.BlockSpec(memory_space=pltpu.VMEM)
    dma = pltpu.SemaphoreType.DMA
    field = pl.pallas_call(
        functools.partial(kernel, dims),
        out_shape=jax.ShapeDtypeStruct((2, n, width), F32),
        in_specs=[anywhere] * 5 + [vmem] * 3 + [pl.BlockSpec(memory_space=pltpu.SMEM)] + [anywhere] * 2,
        out_specs=vmem,
        scratch_shapes=[
            pltpu.VMEM((2, n, width), F32),
            pltpu.VMEM((2, 2, n, width), F32),
            pltpu.VMEM((2, n, width), F32),
            pltpu.VMEM((2, CHUNKS, 2, size, width), F32),
            pltpu.VMEM((2, 4 * n, width), BF16),
            pltpu.VMEM((2, 4 * n, width), BF16),
            pltpu.VMEM((2, CHUNKS, 2, size, 2 * n), F32),
            pltpu.VMEM((2, CHUNKS, nx - 1, 2, size, 2 * n), F32),
            pltpu.VMEM((2, *full), F32),
            pltpu.VMEM((rounds, *full), F32),
            pltpu.VMEM((rounds, *full), F32),
            pltpu.VMEM(full, F32),
            pltpu.VMEM((ny - 1, *full), F32),
            pltpu.VMEM(full, F32),
            pltpu.VMEM(full, F32),
            pltpu.VMEM(full, F32),
            pltpu.VMEM(full, F32),
            pltpu.VMEM(full, F32),
            dma((4,)),
            dma((2, CHUNKS)),
            dma((2, CHUNKS)),
            dma((2, CHUNKS, nx - 1)),
            dma((2, CHUNKS, nx - 1)),
            dma(()),
            dma(()),
            dma((rounds,)),
            dma((rounds,)),
            dma((ny - 1,)),
            dma((ny - 1,)),
            dma(()),
            dma(()),
        ],
        compiler_params=pltpu.CompilerParams(collective_id=0, has_side_effects=True),
        name="sweeps",
    )(sources[0], dexp[0], dproj[0], uexp[0], uproj[0], ddec, udec, active, count, incd, incu)
    return field[None]


def solution(mesh, ny=4):
    depth, nx = mesh.shape["depth"], mesh.shape["lat"]
    dims = (ny, depth // (2 * ny), nx)
    by_group = P("depth", None, None, "lat")
    return jax.shard_map(
        functools.partial(sweeps, dims),
        mesh=mesh,
        in_specs=(by_group,) * 5
        + (P("depth", None),) * 3
        + (P("depth"),)
        + (P(None, None, "lat"),) * 2,
        out_specs=by_group,
        check_vma=False,
    )
```

time: 194 us -> 46.5 us (0.24)
  the two profiles are of different devices: /device:TPU:8 before, /device:TPU:1 now
where the time goes in v1:
time: 46.5 us; the launch traced here: 46.4 us
  Pallas kernels  43.8 us (94%)
  local copies, waits for them, and re-layouts  1.89 us (4%)
  between operations  0.66 us (1%)
    pallas_call x1, Pallas kernels, sweeps(): pl.pallas_call(functools.partial(kernel, dims), out_shape=jax.ShapeDtypeS...  43.8 us
    unnamed x1, local copies, waits for them, and re-layouts  1.89 us

profile of v1, /device:TPU:1, one launch (start us, length us, event | category | flops | bytes accessed | tf_op | source)
XLA Modules:
  0.0 46.4 jit_solution(18337039220168630873)
XLA Ops:
  0.7 43.8 %sweeps.1 = f32[2,64,1024]{2,1,0:T(8,128)} custom-call(f32[2,64,1024]{2,1,0:T(8,128)} %bitcast.7, f32[2,64,1024]{2,1,0:T(8,128)} %bitcast.8, f32[2,64,1024]{2,1,0:T(8,128)} %bitcast.9, f32[2,64,1024]{2,1,0:T(8,128)} %bitcast.10, f32[2,64,1024]{2,1,0:T(8,128)} %bitcast.11, f32[1,64]{1,0:T(1,128)} %ddec_ref.1, f32[1,64]{1,0:T(1,128)} %udec_ref.1, ...), custom_call_target="tpu_custom_call" | custom-call | tf_op jit(solution)/shard_map/sweeps/pallas_call | solution.py:322
  44.5 1.9 %copy.14 = f32[1,2,64,1024]{3,2,1,0:T(8,128)} copy(f32[1,2,64,1024]{3,2,1,0:T(8,128)} %bitcast.6) | data formatting | bytes 1048576

commit v2 on v1

v2 whole, which is shorter than its diff:
```python
import functools

import jax
import jax.numpy as jnp
from jax import lax
from jax.experimental import pallas as pl
from jax.experimental.pallas import tpu as pltpu
from jax.sharding import PartitionSpec as P

F32 = jnp.float32
BF16 = jnp.bfloat16
MESH = pl.DeviceIdType.MESH
CHUNKS = 4


def halves(value):
    high = value.astype(BF16)
    return high, (value - high.astype(F32)).astype(BF16)


def dot(left, right):
    return lax.dot_general(left, right, (((1,), (0,)), ((), ())), preferred_element_type=F32)


def dot_rows(left, right):
    return lax.dot_general(left, right, (((1,), (1,)), ((), ())), preferred_element_type=F32)


def lanes_of(shape):
    return lax.broadcasted_iota(jnp.int32, shape, 1)


def turn(value):
    n = value.shape[1] // 2
    back = pltpu.roll(value, n, 1)
    return jnp.where(lanes_of(value.shape) < n, -back, back)


def product(left, right):
    l_h, l_l = halves(left)
    r_h, r_l = halves(right)
    out = dot(jnp.concatenate([l_h, l_l], axis=1), jnp.concatenate([r_h, r_h], axis=0))
    return out + dot(l_h, r_l)


def apply(later, offset):
    return product(later[0], jnp.concatenate([offset, turn(offset)], axis=0)) + later[1]


def compose(later, earlier):
    both = jnp.concatenate(earlier, axis=1)
    low = jnp.concatenate([turn(earlier[0]), turn(earlier[1])], axis=1)
    out = product(later[0], jnp.concatenate([both, low], axis=0))
    width = earlier[0].shape[1]
    return out[:, :width], out[:, width:] + later[1]


def select(which, first, second):
    return tuple(jnp.where(which, a, b) for a, b in zip(first, second))


def kernel(
    dims,
    src_hbm, dexp_hbm, dproj_hbm, uexp_hbm, uproj_hbm, ddec_ref, udec_ref, list_ref, count_ref, incd_hbm, incu_hbm,
    out_ref,
    src, exps, inc, pown, near, far, wh, wl, fsend, frecv, ssend, srecv, irecv,
    zsend, zrecv, ysend, yrecv, column, qsend, qrecv,
    load_sem, near_sem, far_send_sem, far_recv_sem, fsend_sem, frecv_sem, ssend_sem, srecv_sem, irecv_sem,
    zsend_sem, zrecv_sem, ysend_sem, yrecv_sem, qsend_sem, qrecv_sem,
):
    ny, nz, nx = dims
    rounds = nz.bit_length() - 1
    masks = [1 << k for k in range(rounds - 1)] + [nz - 1]
    n = src.shape[1]
    size = n // CHUNKS
    width = src.shape[2]
    wide = (n, 2 * n)
    g = lax.axis_index("depth")
    x = lax.axis_index("lat")
    core = lax.rem(g, 2)
    z = lax.rem(lax.div(g, 2), nz)
    y = lax.div(g, 2 * nz)
    mate = g + 1 - 2 * core
    hub = g + 1 - core
    is_hub = core == 1
    sweep = lax.rem(x, 2)
    zz = jnp.where(sweep == 0, z, nz - 1 - z)
    yy = jnp.where(sweep == 0, y, ny - 1 - y)
    begins = jnp.logical_and(yy == 0, zz == 0)
    ends = jnp.logical_and(yy == ny - 1, zz == nz - 1)
    edge = jnp.logical_or(g == 0, g == 2 * ny * nz - 1)
    inner = jnp.logical_not(edge)
    before = jnp.where(edge, g, g - 1 + 2 * core)

    def xor(value, mask):
        out = value
        for bit in range(rounds):
            if mask >> bit & 1:
                out = out + (1 << bit) * (1 - 2 * lax.rem(lax.div(value, 1 << bit), 2))
        return out

    def place(to_y, to_z):
        return (to_y * nz + to_z) * 2 + 1

    z_peers = [place(y, xor(z, mask)) for mask in masks]
    y_peers = [place(jnp.where(sweep == 0, lax.rem(y + o, ny), lax.rem(y + ny - o, ny)), z) for o in range(1, ny)]

    pending = []

    def remote(src_ref, dst_ref, send_sem, recv_sem, to, if_so=None, keep=True):
        copy = pltpu.make_async_remote_copy(
            src_ref=src_ref, dst_ref=dst_ref, send_sem=send_sem, recv_sem=recv_sem,
            device_id=to, device_id_type=MESH,
        )
        if if_so is None:
            copy.start()
        else:
            pl.when(if_so)(copy.start)
        if keep:
            pending.append(copy.wait_send if if_so is None else lambda: pl.when(if_so)(copy.wait_send))
        return copy

    def to_hub(src_ref, dst_ref, send_sem, recv_sem, at, if_so=None):
        itself = jnp.logical_and(is_hub, x == at)
        away = jnp.logical_not(itself)
        if if_so is not None:
            itself, away = jnp.logical_and(itself, if_so), jnp.logical_and(away, if_so)
        copy = remote(src_ref, dst_ref, send_sem, recv_sem, (hub, at), away)
        pl.when(itself)(pltpu.make_async_copy(src_ref, dst_ref, recv_sem).start)
        return copy

    barrier = pltpu.get_barrier_semaphore()

    def greet(group, at):
        pl.semaphore_signal(barrier, inc=1, device_id=(group, at), device_id_type=MESH)

    for o in range(nx):
        greet(mate, lax.rem(x + o, nx))
    pl.when(inner)(lambda: greet(before, x))

    @pl.when(is_hub)
    def _():
        for o in range(1, nx):
            greet(g, lax.rem(x + o, nx))
        for peer in z_peers + y_peers:
            greet(peer, x)

    loads = [
        pltpu.make_async_copy(a, b, load_sem.at[i])
        for i, (a, b) in enumerate(
            [
                (dproj_hbm, pown.at[0]),
                (uproj_hbm, pown.at[1]),
                (dexp_hbm, exps.at[0]),
                (src_hbm, src),
                (uexp_hbm, exps.at[1]),
            ]
        )
    ]
    for copy in loads:
        copy.start()
    inc_copies = [pltpu.make_async_copy(a, inc, load_sem.at[5]) for a in (incd_hbm, incu_hbm)]
    pl.when(jnp.logical_and(edge, core == 0))(inc_copies[0].start)
    pl.when(jnp.logical_and(edge, core == 1))(inc_copies[1].start)

    extra = jnp.where(is_hub, nx - 1 + rounds + ny - 1, 0)
    pl.semaphore_wait(barrier, nx + jnp.where(edge, 0, 1) + extra)

    loads[0].wait()
    loads[1].wait()
    far_copies = []
    for k in range(CHUNKS):
        rows = pl.ds(k * size, size)
        far_copies.append(
            remote(pown.at[core, :, rows], far.at[k], far_send_sem.at[k], far_recv_sem.at[k], (before, x), inner)
        )
        own = pltpu.make_async_copy(pown.at[core, :, rows], far.at[k], far_recv_sem.at[k])
        pl.when(edge)(own.start)
    near_copy = remote(pown.at[1 - core], near, near_sem.at[0], near_sem.at[1], (mate, x))

    square = (n, n)
    row_at = lax.broadcasted_iota(jnp.int32, square, 0)
    lane_at = lanes_of(square)
    valid = jnp.logical_and(list_ref[...] == row_at, lane_at < count_ref[0])
    mask = jnp.sum(jnp.where(valid, 1.0, 0.0), axis=1, keepdims=True)
    for copy in loads[2:]:
        copy.wait()
    for role in range(2):
        first, second = (ddec_ref, udec_ref) if role == 0 else (udec_ref, ddec_ref)
        decay = jnp.where(core == 0, first[...], second[...])
        decay = jnp.sum(jnp.where(row_at == lane_at, decay, 0.0), axis=1, keepdims=True)
        slot = core if role == 0 else 1 - core
        for at in range(2):
            high, low = halves(exps[slot, at] * decay)
            wh[role, pl.ds(at * n, n)] = high
            wl[role, pl.ds(at * n, n)] = low
            high, low = halves(src[at] * mask)
            wh[role, pl.ds((2 + at) * n, n)] = high
            wl[role, pl.ds((2 + at) * n, n)] = low

    @pl.when(edge)
    def _():
        inc_copies[0].wait()
        for at in range(2):
            high, low = halves(inc[at])
            wh[1, pl.ds((2 + at) * n, n)] = high
            wl[1, pl.ds((2 + at) * n, n)] = low

    def meet(right, role):
        rows = right.shape[0] // 2
        p_h, p_l = halves(right)
        both = dot_rows(jnp.concatenate([p_h, p_l], axis=0), wh[role])
        total = both[: 2 * rows] + both[2 * rows :] + dot_rows(p_h, wl[role])
        real, imag = total[:rows], total[rows:]
        return real[:, : 2 * n] + turn(imag[:, : 2 * n]), real[:, 2 * n :] + turn(imag[:, 2 * n :])

    near_copy.wait_recv()
    fsend[0], fsend[1] = meet(near[...].reshape(2 * n, width), 0)
    half = nx // 2
    for j in range(half):
        to_hub(fsend, frecv.at[x], fsend_sem.at[j], frecv_sem.at[x], core + 2 * j)
    for k in range(CHUNKS):
        far_copies[k].wait_recv()
        ssend[k, 0], ssend[k, 1] = meet(far[k].reshape(2 * size, width), 1)
        for j in range(half):
            sem = ssend_sem.at[k, j]
            to_hub(ssend.at[k], srecv.at[k, x], sem, srecv_sem.at[k, x], 1 - core + 2 * j, inner)
            to_hub(ssend.at[k], irecv.at[k, x], sem, irecv_sem.at[k, x], core + 2 * j, edge)

    def arrived(ref, sem):
        pltpu.make_async_copy(ref, ref, sem).wait()

    lane = lanes_of(wide)

    @pl.when(is_hub)
    def _():
        mine = []
        for at in range(nx):
            arrived(frecv.at[at], frecv_sem.at[at])
        for i in range(2):
            total = frecv[0, i]
            for at in range(1, nx):
                total = total + frecv[at, i]
            mine.append(total)
        mine = tuple(mine)

        @pl.when(begins)
        def _():
            totals = []
            for k in range(CHUNKS):
                for at in range(nx):
                    arrived(irecv.at[k, at], irecv_sem.at[k, at])
                total = irecv[k, 0, 1]
                for at in range(1, nx):
                    total = total + irecv[k, at, 1]
                totals.append(total)
            column[0] = jnp.concatenate(totals, axis=0)
            column[1] = apply(mine, column[0])

        first = select(begins, (jnp.zeros(wide, F32), column[1]), mine)

        @pl.when(jnp.logical_not(ends))
        def _():
            parts = [[], []]
            for k in range(CHUNKS):
                for at in range(nx):
                    arrived(srecv.at[k, at], srecv_sem.at[k, at])
                for i in range(2):
                    total = srecv[k, 0, i]
                    for at in range(1, nx):
                        total = total + srecv[k, at, i]
                    parts[i].append(total)
            theirs = tuple(jnp.concatenate(p, axis=0) for p in parts)
            zsend[0, 0], zsend[0, 1] = compose(theirs, first)

        @pl.when(ends)
        def _():
            zsend[0] = jnp.zeros(zsend.shape[1:], F32)

        row = lax.broadcasted_iota(jnp.int32, wide, 0)
        prefix = (jnp.where(row == lane, 1.0, 0.0), jnp.zeros(wide, F32))
        waits = []
        for k in range(rounds):
            copy = remote(
                zsend.at[k], zrecv.at[k], zsend_sem.at[k], zrecv_sem.at[k], (z_peers[k], x), keep=False
            )
            waits.append(copy.wait_send)
            total = (zsend[k, 0], zsend[k, 1])
            copy.wait_recv()
            theirs = (zrecv[k, 0], zrecv[k, 1])
            after = lax.rem(lax.div(zz, 1 << k), 2) == 1
            both = compose(select(after, total, theirs), select(after, theirs, total))
            to = zsend.at[k + 1] if k + 1 < rounds else ysend
            to[0], to[1] = both
            prefix = select(after, compose(prefix, theirs) if k else theirs, prefix)

        y_copies, y_firsts = [], []
        for o in range(1, ny):
            to = (y_peers[o - 1], x)
            sems = (ysend_sem.at[o - 1], yrecv_sem.at[o - 1])
            whole = jnp.logical_and(yy > 0, yy + o < ny)
            y_copies.append(remote(ysend, yrecv.at[o - 1], *sems, to, whole, keep=False))
            y_firsts.append(remote(ysend.at[1], yrecv.at[o - 1, 1], *sems, to, yy == 0, keep=False))
            waits.append(lambda c=y_copies[-1], w=whole: pl.when(w)(c.wait_send))
            waits.append(lambda c=y_firsts[-1]: pl.when(yy == 0)(c.wait_send))

        @pl.when(yy == 0)
        def _():
            qsend[0] = jnp.where(begins, column[0], prefix[1])

        for at in range(1, ny):

            @pl.when(yy == at)
            def _():
                y_firsts[at - 1].wait_recv()
                here = yrecv[at - 1, 1]
                for o in range(at - 1, 0, -1):
                    y_copies[o - 1].wait_recv()
                    here = apply((yrecv[o - 1, 0], yrecv[o - 1, 1]), here)
                qsend[0] = apply(prefix, here)

        beside = x + 1 - 2 * sweep
        chip = g - 1
        for i in range(2):
            if i == 1:
                qsend[1] = apply(mine, qsend[0])
            which = sweep if i == 0 else 1 - sweep
            sems = [(qsend_sem.at[i, j], qrecv_sem.at[sweep]) for j in range(2)]
            copy = remote(qsend.at[i], qrecv.at[sweep], *sems[0], (chip + which, beside), keep=False)
            waits.append(copy.wait_send)
            here = which == 0
            copy = remote(qsend.at[i], qrecv.at[sweep], *sems[1], (chip, x), here, keep=False)
            waits.append(lambda c=copy, w=here: pl.when(w)(c.wait_send))
            own = pltpu.make_async_copy(qsend.at[i], qrecv.at[sweep], qrecv_sem.at[sweep])
            pl.when(which == 1)(own.start)
        for wait in waits:
            wait()

    for at, decay in enumerate((ddec_ref[...], udec_ref[...])):
        arrived(qrecv.at[at], qrecv_sem.at[at])
        columns = qrecv[at]
        turned = jnp.transpose(jnp.concatenate([columns, pltpu.roll(columns, n, 1)], axis=0))[:n]
        out_ref[at] = turned * jnp.concatenate([decay, decay], axis=1)
    for wait in pending:
        wait()


def add_terms(dexp, uexp, src, coef, list_ref, count_ref, out_hbm, field, sems):
    _, n, width = src.shape
    square = (n, n)
    valid = jnp.logical_and(
        list_ref[...] == lax.broadcasted_iota(jnp.int32, square, 0), lanes_of(square) < count_ref[0]
    )
    mask = jnp.sum(jnp.where(valid, 1.0, 0.0), axis=1, keepdims=True)
    parts = []
    for sweep in range(2):
        value = coef[sweep]
        left = lanes_of(value.shape) < n
        parts.append(jnp.concatenate([jnp.where(left, value, -value), pltpu.roll(value, n, 1)], axis=0))
    c_h, c_l = halves(jnp.concatenate(parts, axis=1))
    c_all = jnp.concatenate([c_h, c_l], axis=0)
    step = min(256, width)
    copies = []
    for k in range(width // step):
        cols = pl.ds(k * step, step)
        e_h, e_l = halves(
            jnp.concatenate([dexp[:, :, cols].reshape(2 * n, step), uexp[:, :, cols].reshape(2 * n, step)], axis=0)
        )
        both = dot(c_all, e_h)
        terms = both[: 2 * n] + both[2 * n :] + dot(c_h, e_l)
        for i in range(2):
            field[i, :, cols] = src[i, :, cols] * mask + terms[i * n : (i + 1) * n]
        copies.append(pltpu.make_async_copy(field.at[:, :, cols], out_hbm.at[:, :, cols], sems.at[k]))
        copies[-1].start()
    for copy in copies:
        copy.wait()


def sweeps(dims, *args):
    sources, dexp, dproj, uexp, uproj, ddec, udec, active, count, incd, incu = args
    ny, nz, nx = dims
    _, _, n, width = sources.shape
    size = n // CHUNKS
    rounds = nz.bit_length() - 1
    block = (n, 2 * n)
    hbm = pl.BlockSpec(memory_space=pltpu.HBM)
    vmem = pl.BlockSpec(memory_space=pltpu.VMEM)
    smem = pl.BlockSpec(memory_space=pltpu.SMEM)
    dma = pltpu.SemaphoreType.DMA
    coef = pl.pallas_call(
        functools.partial(kernel, dims),
        out_shape=jax.ShapeDtypeStruct((2, *block), F32),
        in_specs=[hbm] * 5 + [vmem] * 3 + [smem] + [hbm] * 2,
        out_specs=vmem,
        scratch_shapes=[
            pltpu.VMEM((2, n, width), F32),
            pltpu.VMEM((2, 2, n, width), F32),
            pltpu.VMEM((2, n, width), F32),
            pltpu.VMEM((2, 2, n, width), F32),
            pltpu.VMEM((2, n, width), F32),
            pltpu.VMEM((CHUNKS, 2, size, width), F32),
            pltpu.VMEM((2, 4 * n, width), BF16),
            pltpu.VMEM((2, 4 * n, width), BF16),
            pltpu.VMEM((2, *block), F32),
            pltpu.VMEM((nx, 2, *block), F32),
            pltpu.VMEM((CHUNKS, 2, size, 2 * n), F32),
            pltpu.VMEM((CHUNKS, nx, 2, size, 2 * n), F32),
            pltpu.VMEM((CHUNKS, nx, 2, size, 2 * n), F32),
            pltpu.VMEM((rounds, 2, *block), F32),
            pltpu.VMEM((rounds, 2, *block), F32),
            pltpu.VMEM((2, *block), F32),
            pltpu.VMEM((ny - 1, 2, *block), F32),
            pltpu.VMEM((2, *block), F32),
            pltpu.VMEM((2, *block), F32),
            pltpu.VMEM((2, *block), F32),
            dma((6,)),
            dma((2,)),
            dma((CHUNKS,)),
            dma((CHUNKS,)),
            dma((nx // 2,)),
            dma((nx,)),
            dma((CHUNKS, nx // 2)),
            dma((CHUNKS, nx)),
            dma((CHUNKS, nx)),
            dma((rounds,)),
            dma((rounds,)),
            dma((ny - 1,)),
            dma((ny - 1,)),
            dma((2, 2)),
            dma((2,)),
        ],
        compiler_params=pltpu.CompilerParams(
            collective_id=0, has_side_effects=True
        ),
        name="sweeps",
    )(sources[0], dexp[0], dproj[0], uexp[0], uproj[0], ddec, udec, active, count, incd, incu)
    field = pl.pallas_call(
        add_terms,
        out_shape=jax.ShapeDtypeStruct((2, n, width), F32),
        in_specs=[vmem] * 5 + [smem],
        out_specs=hbm,
        scratch_shapes=[pltpu.VMEM((2, n, width), F32), dma((max(1, width // 256),))],

        name="add_terms",
    )(dexp[0], uexp[0], sources[0], coef, active, count)
    return field[None]


def solution(mesh, ny=4):
    depth, nx = mesh.shape["depth"], mesh.shape["lat"]
    dims = (ny, depth // (2 * ny), nx)
    by_group = P("depth", None, None, "lat")
    return jax.shard_map(
        functools.partial(sweeps, dims),
        mesh=mesh,
        in_specs=(by_group,) * 5
        + (P("depth", None),) * 3
        + (P("depth"),)
        + (P(None, None, "lat"),) * 2,
        out_specs=by_group,
        check_vma=False,
    )
```

time: 46.5 us -> 42.6 us (0.916)
  Pallas kernels: 43.8 us -> 41.8 us
  local copies, waits for them, and re-layouts: 1.89 us -> 0 us
    pallas_call x1, Pallas kernels: 43.8 us -> 39.3 us  [sweeps(): pl.pallas_call(functools.partial(kernel, dims), out_shape=jax.ShapeDtypeS...]
    pallas_call x0 -> x1, Pallas kernels: none -> 2.52 us  [sweeps(): pl.pallas_call(add_terms, out_shape=jax.ShapeDtypeStruct((2, n, width), F...]
    unnamed x1 -> x0, local copies, waits for them, and re-layouts: 1.89 us -> none
where the time goes in v2:
time: 42.6 us; the launch traced here: 42.4 us
  Pallas kernels  41.8 us (98%)
  between operations  0.66 us (2%)
    pallas_call x1, Pallas kernels, sweeps(): pl.pallas_call(functools.partial(kernel, dims), out_shape=jax.ShapeDtypeS...  39.3 us
    pallas_call x1, Pallas kernels, sweeps(): pl.pallas_call(add_terms, out_shape=jax.ShapeDtypeStruct((2, n, width), F...  2.52 us

profile of v2, /device:TPU:1, one launch (start us, length us, event | category | flops | bytes accessed | tf_op | source)
XLA Modules:
  0.0 42.4 jit_solution(3522489139578048062)
XLA Ops:
  0.7 39.3 %sweeps.1.coef = f32[2,64,128]{2,1,0:T(8,128)} custom-call(f32[2,64,1024]{2,1,0:T(8,128)} %bitcast.10, f32[2,64,1024]{2,1,0:T(8,128)} %bitcast.6, f32[2,64,1024]{2,1,0:T(8,128)} %bitcast.12, f32[2,64,1024]{2,1,0:T(8,128)} %bitcast.8, f32[2,64,1024]{2,1,0:T(8,128)} %bitcast.13, f32[1,64]{1,0:T(1,128)} %ddec_ref.1, f32[1,64]{1,0:T(1,128)} %udec_ref.1, ...), custom_call_target="tpu_custom_call" | custom-call | tf_op jit(solution)/shard_map/sweeps/pallas_call | solution.py:390
  39.9 2.5 %add_terms.1 = f32[2,64,1024]{2,1,0:T(8,128)} custom-call(f32[2,64,1024]{2,1,0:T(8,128)} %bitcast.7, f32[2,64,1024]{2,1,0:T(8,128)} %bitcast.9, f32[2,64,1024]{2,1,0:T(8,128)} %bitcast.11, f32[2,64,128]{2,1,0:T(8,128)} %sweeps.1.coef, s32[1,64]{1,0:T(1,128)} %list_ref.3, s32[1]{0:T(128)S(6)} %copy.12.count_ref), custom_call_target="tpu_custom_call" | custom-call | tf_op jit(solution)/shard_map/add_terms/pallas_call | solution.py:437

commit v3 on v2

--- a/solution.py
+++ b/solution.py
@@ -61,10 +61,10 @@
 
 def kernel(
     dims,
-    src_hbm, dexp_hbm, dproj_hbm, uexp_hbm, uproj_hbm, ddec_ref, udec_ref, list_ref, count_ref, incd_hbm, incu_hbm,
+    src_hbm, dexp_hbm, dproj_hbm, uexp_hbm, uproj_hbm, ddec_hbm, udec_hbm, list_hbm, count_ref, incd_hbm, incu_hbm,
     out_ref,
     src, exps, inc, pown, near, far, wh, wl, fsend, frecv, ssend, srecv, irecv,
-    zsend, zrecv, ysend, yrecv, column, qsend, qrecv,
+    zsend, zrecv, ysend, yrecv, column, qsend, qrecv, ddec_ref, udec_ref, list_ref,
     load_sem, near_sem, far_send_sem, far_recv_sem, fsend_sem, frecv_sem, ssend_sem, srecv_sem, irecv_sem,
     zsend_sem, zrecv_sem, ysend_sem, yrecv_sem, qsend_sem, qrecv_sem,
 ):
@@ -154,12 +154,15 @@
                 (dexp_hbm, exps.at[0]),
                 (src_hbm, src),
                 (uexp_hbm, exps.at[1]),
+                (ddec_hbm, ddec_ref),
+                (udec_hbm, udec_ref),
+                (list_hbm, list_ref),
             ]
         )
     ]
     for copy in loads:
         copy.start()
-    inc_copies = [pltpu.make_async_copy(a, inc, load_sem.at[5]) for a in (incd_hbm, incu_hbm)]
+    inc_copies = [pltpu.make_async_copy(a, inc, load_sem.at[8]) for a in (incd_hbm, incu_hbm)]
     pl.when(jnp.logical_and(edge, core == 0))(inc_copies[0].start)
     pl.when(jnp.logical_and(edge, core == 1))(inc_copies[1].start)
 
@@ -178,13 +181,13 @@
         pl.when(edge)(own.start)
     near_copy = remote(pown.at[1 - core], near, near_sem.at[0], near_sem.at[1], (mate, x))
 
+    for copy in loads[2:]:
+        copy.wait()
     square = (n, n)
     row_at = lax.broadcasted_iota(jnp.int32, square, 0)
     lane_at = lanes_of(square)
     valid = jnp.logical_and(list_ref[...] == row_at, lane_at < count_ref[0])
     mask = jnp.sum(jnp.where(valid, 1.0, 0.0), axis=1, keepdims=True)
-    for copy in loads[2:]:
-        copy.wait()
     for role in range(2):
         first, second = (ddec_ref, udec_ref) if role == 0 else (udec_ref, ddec_ref)
         decay = jnp.where(core == 0, first[...], second[...])
@@ -387,10 +390,11 @@
     vmem = pl.BlockSpec(memory_space=pltpu.VMEM)
     smem = pl.BlockSpec(memory_space=pltpu.SMEM)
     dma = pltpu.SemaphoreType.DMA
+    operands = (sources[0], dexp[0], dproj[0], uexp[0], uproj[0], ddec, udec, active, count, incd, incu)
     coef = pl.pallas_call(
         functools.partial(kernel, dims),
         out_shape=jax.ShapeDtypeStruct((2, *block), F32),
-        in_specs=[hbm] * 5 + [vmem] * 3 + [smem] + [hbm] * 2,
+        in_specs=[hbm] * 8 + [smem] + [hbm] * 2,
         out_specs=vmem,
         scratch_shapes=[
             pltpu.VMEM((2, n, width), F32),
@@ -413,7 +417,10 @@
             pltpu.VMEM((2, *block), F32),
             pltpu.VMEM((2, *block), F32),
             pltpu.VMEM((2, *block), F32),
-            dma((6,)),
+            pltpu.VMEM((1, n), F32),
+            pltpu.VMEM((1, n), F32),
+            pltpu.VMEM((1, n), jnp.int32),
+            dma((9,)),
             dma((2,)),
             dma((CHUNKS,)),
             dma((CHUNKS,)),
@@ -430,10 +437,10 @@
             dma((2,)),
         ],
         compiler_params=pltpu.CompilerParams(
-            collective_id=0, has_side_effects=True
+            collective_id=0, has_side_effects=True, vmem_limit_bytes=24 * 2**20
         ),
         name="sweeps",
-    )(sources[0], dexp[0], dproj[0], uexp[0], uproj[0], ddec, udec, active, count, incd, incu)
+    )(*(v if v is count else pltpu.with_memory_space_constraint(v, pltpu.HBM) for v in operands))
     field = pl.pallas_call(
         add_terms,
         out_shape=jax.ShapeDtypeStruct((2, n, width), F32),
@@ -441,6 +448,7 @@
         out_specs=hbm,
         scratch_shapes=[pltpu.VMEM((2, n, width), F32), dma((max(1, width // 256),))],
 
+        compiler_params=pltpu.CompilerParams(vmem_limit_bytes=16 * 2**20),
         name="add_terms",
     )(dexp[0], uexp[0], sources[0], coef, active, count)
     return field[None]

time: 42.6 us -> 40 us (0.939)
  Pallas kernels: 41.8 us -> 39.2 us
    pallas_call x1, Pallas kernels: 2.52 us -> 1.14 us  [sweeps(): pl.pallas_call(add_terms, out_shape=jax.ShapeDtypeStruct((2, n, width), F...]
    pallas_call x1, Pallas kernels: 39.3 us -> 38 us  [sweeps(): pl.pallas_call(functools.partial(kernel, dims), out_shape=jax.ShapeDtypeS...]
where the time goes in v3:
time: 40 us; the launch traced here: 39.9 us
  Pallas kernels  39.2 us (98%)
  between operations  0.72 us (2%)
    pallas_call x1, Pallas kernels, sweeps(): pl.pallas_call(functools.partial(kernel, dims), out_shape=jax.ShapeDtypeS...  38 us
    pallas_call x1, Pallas kernels, sweeps(): pl.pallas_call(add_terms, out_shape=jax.ShapeDtypeStruct((2, n, width), F...  1.14 us

profile of v3, /device:TPU:1, one launch (start us, length us, event | category | flops | bytes accessed | tf_op | source)
XLA Modules:
  0.0 39.9 jit_solution(18166375774024284901)
XLA Ops:
  0.7 0.0 copy-start
  0.7 0.0 copy-start.1
  0.7 0.0 copy-start.2
  0.7 0.0 copy-start.3
  0.7 38.0 %sweeps.1.coef = f32[2,64,128]{2,1,0:T(8,128)S(1)} custom-call(f32[2,64,1024]{2,1,0:T(8,128)} %bitcast.10, f32[2,64,1024]{2,1,0:T(8,128)} %bitcast.6, f32[2,64,1024]{2,1,0:T(8,128)} %bitcast.12, f32[2,64,1024]{2,1,0:T(8,128)} %bitcast.8, f32[2,64,1024]{2,1,0:T(8,128)} %bitcast.13, f32[1,64]{1,0:T(1,128)} %ddec_hbm.1, f32[1,64]{1,0:T(1,128)} %udec_hbm.1, ...), custom_call_target="tpu_custom_call" | custom-call | tf_op jit(solution)/shard_map/sweeps/pallas_call | solution.py:394
  38.7 0.0 copy-done
  38.8 0.0 copy-done.1
  38.8 0.0 copy-done.2
  38.8 0.0 copy-done.3
  38.8 1.1 %add_terms.1 = f32[2,64,1024]{2,1,0:T(8,128)} custom-call(f32[2,64,1024]{2,1,0:T(8,128)S(1)} %bitcast.7, f32[2,64,1024]{2,1,0:T(8,128)S(1)} %bitcast.9, f32[2,64,1024]{2,1,0:T(8,128)S(1)} %bitcast.11, f32[2,64,128]{2,1,0:T(8,128)S(1)} %sweeps.1.coef, s32[1,64]{1,0:T(1,128)S(1)} %copy-done.3, s32[1]{0:T(128)S(6)} %copy.12.count_ref), custom_call_target="tpu_custom_call" | custom-call | tf_op jit(solution)/shard_map/add_terms/pallas_call | solution.py:444
Async XLA Ops:
  0.7 38.1 %copy-start = (f32[1,2,64,1024]{3,2,1,0:T(8,128)S(1)}, f32[1,2,64,1024]{3,2,1,0:T(8,128)}, u32[]{:S(2)}) copy-start(f32[1,2,64,1024]{3,2,1,0:T(8,128)} %param.12) | copy-start | bytes 1572868
  0.7 38.1 %copy-start.1 = (f32[1,2,64,1024]{3,2,1,0:T(8,128)S(1)}, f32[1,2,64,1024]{3,2,1,0:T(8,128)}, u32[]{:S(2)}) copy-start(f32[1,2,64,1024]{3,2,1,0:T(8,128)} %param.14) | copy-start | bytes 1572868
  0.7 38.1 %copy-start.2 = (f32[1,2,64,1024]{3,2,1,0:T(8,128)S(1)}, f32[1,2,64,1024]{3,2,1,0:T(8,128)}, u32[]{:S(2)}) copy-start(f32[1,2,64,1024]{3,2,1,0:T(8,128)} %param.11) | copy-start | bytes 1572868
  0.7 38.1 %copy-start.3 = (s32[1,64]{1,0:T(1,128)S(1)}, s32[1,64]{1,0:T(1,128)}, u32[]{:S(2)}) copy-start(s32[1,64]{1,0:T(1,128)} %list_ref.1) | copy-start | bytes 772

commit v4 on v3

--- a/solution.py
+++ b/solution.py
@@ -83,7 +83,7 @@
     mate = g + 1 - 2 * core
     hub = g + 1 - core
     is_hub = core == 1
-    sweep = lax.rem(x, 2)
+    sweep = lax.rem(x + 1, 2)
     zz = jnp.where(sweep == 0, z, nz - 1 - z)
     yy = jnp.where(sweep == 0, y, ny - 1 - y)
     begins = jnp.logical_and(yy == 0, zz == 0)
@@ -221,14 +221,14 @@
     fsend[0], fsend[1] = meet(near[...].reshape(2 * n, width), 0)
     half = nx // 2
     for j in range(half):
-        to_hub(fsend, frecv.at[x], fsend_sem.at[j], frecv_sem.at[x], core + 2 * j)
+        to_hub(fsend, frecv.at[x], fsend_sem.at[j], frecv_sem.at[x], 1 - core + 2 * j)
     for k in range(CHUNKS):
         far_copies[k].wait_recv()
         ssend[k, 0], ssend[k, 1] = meet(far[k].reshape(2 * size, width), 1)
         for j in range(half):
             sem = ssend_sem.at[k, j]
-            to_hub(ssend.at[k], srecv.at[k, x], sem, srecv_sem.at[k, x], 1 - core + 2 * j, inner)
-            to_hub(ssend.at[k], irecv.at[k, x], sem, irecv_sem.at[k, x], core + 2 * j, edge)
+            to_hub(ssend.at[k], srecv.at[k, x], sem, srecv_sem.at[k, x], core + 2 * j, inner)
+            to_hub(ssend.at[k], irecv.at[k, x], sem, irecv_sem.at[k, x], 1 - core + 2 * j, edge)
 
     def arrived(ref, sem):
         pltpu.make_async_copy(ref, ref, sem).wait()
@@ -283,29 +283,40 @@
         row = lax.broadcasted_iota(jnp.int32, wide, 0)
         prefix = (jnp.where(row == lane, 1.0, 0.0), jnp.zeros(wide, F32))
         waits = []
-        for k in range(rounds):
+
+        def pass_on(k):
             copy = remote(
                 zsend.at[k], zrecv.at[k], zsend_sem.at[k], zrecv_sem.at[k], (z_peers[k], x), keep=False
             )
             waits.append(copy.wait_send)
+            return copy
+
+        y_copies, y_firsts = {}, {}
+
+        def pass_down():
+            for o in range(ny - 1, 0, -1):
+                to = (y_peers[o - 1], x)
+                sems = (ysend_sem.at[o - 1], yrecv_sem.at[o - 1])
+                whole = jnp.logical_and(yy > 0, yy + o < ny)
+                y_copies[o] = remote(ysend, yrecv.at[o - 1], *sems, to, whole, keep=False)
+                y_firsts[o] = remote(ysend.at[1], yrecv.at[o - 1, 1], *sems, to, yy == 0, keep=False)
+                waits.append(lambda c=y_copies[o], w=whole: pl.when(w)(c.wait_send))
+                waits.append(lambda c=y_firsts[o]: pl.when(yy == 0)(c.wait_send))
+
+        copy = pass_on(0)
+        for k in range(rounds):
             total = (zsend[k, 0], zsend[k, 1])
             copy.wait_recv()
             theirs = (zrecv[k, 0], zrecv[k, 1])
             after = lax.rem(lax.div(zz, 1 << k), 2) == 1
             both = compose(select(after, total, theirs), select(after, theirs, total))
-            to = zsend.at[k + 1] if k + 1 < rounds else ysend
-            to[0], to[1] = both
+            if k + 1 < rounds:
+                zsend[k + 1, 0], zsend[k + 1, 1] = both
+                copy = pass_on(k + 1)
+            else:
+                ysend[0], ysend[1] = both
+                pass_down()
             prefix = select(after, compose(prefix, theirs) if k else theirs, prefix)
-
-        y_copies, y_firsts = [], []
-        for o in range(1, ny):
-            to = (y_peers[o - 1], x)
-            sems = (ysend_sem.at[o - 1], yrecv_sem.at[o - 1])
-            whole = jnp.logical_and(yy > 0, yy + o < ny)
-            y_copies.append(remote(ysend, yrecv.at[o - 1], *sems, to, whole, keep=False))
-            y_firsts.append(remote(ysend.at[1], yrecv.at[o - 1, 1], *sems, to, yy == 0, keep=False))
-            waits.append(lambda c=y_copies[-1], w=whole: pl.when(w)(c.wait_send))
-            waits.append(lambda c=y_firsts[-1]: pl.when(yy == 0)(c.wait_send))
 
         @pl.when(yy == 0)
         def _():
@@ -315,14 +326,18 @@
 
             @pl.when(yy == at)
             def _():
-                y_firsts[at - 1].wait_recv()
+                last = prefix
+                if at > 2:
+                    y_copies[1].wait_recv()
+                    last = compose(prefix, (yrecv[0, 0], yrecv[0, 1]))
+                y_firsts[at].wait_recv()
                 here = yrecv[at - 1, 1]
-                for o in range(at - 1, 0, -1):
-                    y_copies[o - 1].wait_recv()
+                for o in range(at - 1, 0 if at <= 2 else 1, -1):
+                    y_copies[o].wait_recv()
                     here = apply((yrecv[o - 1, 0], yrecv[o - 1, 1]), here)
-                qsend[0] = apply(prefix, here)
-
-        beside = x + 1 - 2 * sweep
+                qsend[0] = apply(last, here)
+
+        beside = x - 1 + 2 * sweep
         chip = g - 1
         for i in range(2):
             if i == 1:

time: 40 us -> 39.5 us (0.988)
  Pallas kernels: 39.2 us -> 38.7 us
    pallas_call x1, Pallas kernels: 38 us -> 37.6 us  [sweeps(): pl.pallas_call(functools.partial(kernel, dims), out_shape=jax.ShapeDtypeS...]
where the time goes in v4:
time: 39.5 us; the launch traced here: 39.4 us
  Pallas kernels  38.7 us (98%)
  between operations  0.72 us (2%)
    pallas_call x1, Pallas kernels, sweeps(): pl.pallas_call(functools.partial(kernel, dims), out_shape=jax.ShapeDtypeS...  37.6 us
    pallas_call x1, Pallas kernels, sweeps(): pl.pallas_call(add_terms, out_shape=jax.ShapeDtypeStruct((2, n, width), F...  1.14 us

profile of v4, /device:TPU:1, one launch (start us, length us, event | category | flops | bytes accessed | tf_op | source)
XLA Modules:
  0.0 39.4 jit_solution(12318819255199252830)
XLA Ops:
  0.7 0.0 copy-start
  0.7 0.0 copy-start.1
  0.7 0.0 copy-start.2
  0.7 0.0 copy-start.3
  0.7 37.6 %sweeps.1.coef = f32[2,64,128]{2,1,0:T(8,128)S(1)} custom-call(f32[2,64,1024]{2,1,0:T(8,128)} %bitcast.10, f32[2,64,1024]{2,1,0:T(8,128)} %bitcast.6, f32[2,64,1024]{2,1,0:T(8,128)} %bitcast.12, f32[2,64,1024]{2,1,0:T(8,128)} %bitcast.8, f32[2,64,1024]{2,1,0:T(8,128)} %bitcast.13, f32[1,64]{1,0:T(1,128)} %ddec_hbm.1, f32[1,64]{1,0:T(1,128)} %udec_hbm.1, ...), custom_call_target="tpu_custom_call" | custom-call | tf_op jit(solution)/shard_map/sweeps/pallas_call | solution.py:409
  38.3 0.0 copy-done
  38.3 0.0 copy-done.1
  38.3 0.0 copy-done.2
  38.3 0.0 copy-done.3
  38.3 1.1 %add_terms.1 = f32[2,64,1024]{2,1,0:T(8,128)} custom-call(f32[2,64,1024]{2,1,0:T(8,128)S(1)} %bitcast.7, f32[2,64,1024]{2,1,0:T(8,128)S(1)} %bitcast.9, f32[2,64,1024]{2,1,0:T(8,128)S(1)} %bitcast.11, f32[2,64,128]{2,1,0:T(8,128)S(1)} %sweeps.1.coef, s32[1,64]{1,0:T(1,128)S(1)} %copy-done.3, s32[1]{0:T(128)S(6)} %copy.12.count_ref), custom_call_target="tpu_custom_call" | custom-call | tf_op jit(solution)/shard_map/add_terms/pallas_call | solution.py:459
Async XLA Ops:
  0.7 37.6 %copy-start = (f32[1,2,64,1024]{3,2,1,0:T(8,128)S(1)}, f32[1,2,64,1024]{3,2,1,0:T(8,128)}, u32[]{:S(2)}) copy-start(f32[1,2,64,1024]{3,2,1,0:T(8,128)} %param.12) | copy-start | bytes 1572868
  0.7 37.6 %copy-start.1 = (f32[1,2,64,1024]{3,2,1,0:T(8,128)S(1)}, f32[1,2,64,1024]{3,2,1,0:T(8,128)}, u32[]{:S(2)}) copy-start(f32[1,2,64,1024]{3,2,1,0:T(8,128)} %param.14) | copy-start | bytes 1572868
  0.7 37.6 %copy-start.2 = (f32[1,2,64,1024]{3,2,1,0:T(8,128)S(1)}, f32[1,2,64,1024]{3,2,1,0:T(8,128)}, u32[]{:S(2)}) copy-start(f32[1,2,64,1024]{3,2,1,0:T(8,128)} %param.11) | copy-start | bytes 1572868
  0.7 37.6 %copy-start.3 = (s32[1,64]{1,0:T(1,128)S(1)}, s32[1,64]{1,0:T(1,128)}, u32[]{:S(2)}) copy-start(s32[1,64]{1,0:T(1,128)} %list_ref.1) | copy-start | bytes 772

commit v5 on v4

--- a/solution.py
+++ b/solution.py
@@ -70,7 +70,7 @@
 ):
     ny, nz, nx = dims
     rounds = nz.bit_length() - 1
-    masks = [1 << k for k in range(rounds - 1)] + [nz - 1]
+    masks = [(2 << k) - 1 for k in range(rounds)]
     n = src.shape[1]
     size = n // CHUNKS
     width = src.shape[2]

time: 39.5 us -> 39 us (0.987)
  Pallas kernels: 38.7 us -> 38.1 us
    pallas_call x1, Pallas kernels: 37.6 us -> 37 us  [sweeps(): pl.pallas_call(functools.partial(kernel, dims), out_shape=jax.ShapeDtypeS...]
where the time goes in v5:
time: 39 us; the launch traced here: 38.9 us
  Pallas kernels  38.1 us (98%)
  between operations  0.72 us (2%)
    pallas_call x1, Pallas kernels, sweeps(): pl.pallas_call(functools.partial(kernel, dims), out_shape=jax.ShapeDtypeS...  37 us
    pallas_call x1, Pallas kernels, sweeps(): pl.pallas_call(add_terms, out_shape=jax.ShapeDtypeStruct((2, n, width), F...  1.14 us

profile of v5, /device:TPU:1, one launch (start us, length us, event | category | flops | bytes accessed | tf_op | source)
XLA Modules:
  0.0 38.9 jit_solution(18334032022720719521)
XLA Ops:
  0.7 0.0 copy-start
  0.7 0.0 copy-start.1
  0.7 0.0 copy-start.2
  0.7 0.0 copy-start.3
  0.7 37.0 %sweeps.1.coef = f32[2,64,128]{2,1,0:T(8,128)S(1)} custom-call(f32[2,64,1024]{2,1,0:T(8,128)} %bitcast.10, f32[2,64,1024]{2,1,0:T(8,128)} %bitcast.6, f32[2,64,1024]{2,1,0:T(8,128)} %bitcast.12, f32[2,64,1024]{2,1,0:T(8,128)} %bitcast.8, f32[2,64,1024]{2,1,0:T(8,128)} %bitcast.13, f32[1,64]{1,0:T(1,128)} %ddec_hbm.1, f32[1,64]{1,0:T(1,128)} %udec_hbm.1, ...), custom_call_target="tpu_custom_call" | custom-call | tf_op jit(solution)/shard_map/sweeps/pallas_call | solution.py:409
  37.7 0.0 copy-done
  37.7 0.0 copy-done.1
  37.7 0.0 copy-done.2
  37.7 0.0 copy-done.3
  37.7 1.1 %add_terms.1 = f32[2,64,1024]{2,1,0:T(8,128)} custom-call(f32[2,64,1024]{2,1,0:T(8,128)S(1)} %bitcast.7, f32[2,64,1024]{2,1,0:T(8,128)S(1)} %bitcast.9, f32[2,64,1024]{2,1,0:T(8,128)S(1)} %bitcast.11, f32[2,64,128]{2,1,0:T(8,128)S(1)} %sweeps.1.coef, s32[1,64]{1,0:T(1,128)S(1)} %copy-done.3, s32[1]{0:T(128)S(6)} %copy.12.count_ref), custom_call_target="tpu_custom_call" | custom-call | tf_op jit(solution)/shard_map/add_terms/pallas_call | solution.py:459
Async XLA Ops:
  0.7 37.0 %copy-start = (f32[1,2,64,1024]{3,2,1,0:T(8,128)S(1)}, f32[1,2,64,1024]{3,2,1,0:T(8,128)}, u32[]{:S(2)}) copy-start(f32[1,2,64,1024]{3,2,1,0:T(8,128)} %param.12) | copy-start | bytes 1572868
  0.7 37.0 %copy-start.1 = (f32[1,2,64,1024]{3,2,1,0:T(8,128)S(1)}, f32[1,2,64,1024]{3,2,1,0:T(8,128)}, u32[]{:S(2)}) copy-start(f32[1,2,64,1024]{3,2,1,0:T(8,128)} %param.14) | copy-start | bytes 1572868
  0.7 37.0 %copy-start.2 = (f32[1,2,64,1024]{3,2,1,0:T(8,128)S(1)}, f32[1,2,64,1024]{3,2,1,0:T(8,128)}, u32[]{:S(2)}) copy-start(f32[1,2,64,1024]{3,2,1,0:T(8,128)} %param.11) | copy-start | bytes 1572868
  0.7 37.0 %copy-start.3 = (s32[1,64]{1,0:T(1,128)S(1)}, s32[1,64]{1,0:T(1,128)}, u32[]{:S(2)}) copy-start(s32[1,64]{1,0:T(1,128)} %list_ref.1) | copy-start | bytes 772

commit v6 on v5

--- a/solution.py
+++ b/solution.py
@@ -233,6 +233,13 @@
     def arrived(ref, sem):
         pltpu.make_async_copy(ref, ref, sem).wait()
 
+    def hand_over():
+        for at, decay in enumerate((ddec_ref[...], udec_ref[...])):
+            arrived(qrecv.at[at], qrecv_sem.at[at])
+            columns = qrecv[at]
+            turned = jnp.transpose(jnp.concatenate([columns, pltpu.roll(columns, n, 1)], axis=0))[:n]
+            out_ref[at] = turned * jnp.concatenate([decay, decay], axis=1)
+
     lane = lanes_of(wide)
 
     @pl.when(is_hub)
@@ -351,14 +358,11 @@
             waits.append(lambda c=copy, w=here: pl.when(w)(c.wait_send))
             own = pltpu.make_async_copy(qsend.at[i], qrecv.at[sweep], qrecv_sem.at[sweep])
             pl.when(which == 1)(own.start)
+        hand_over()
         for wait in waits:
             wait()
 
-    for at, decay in enumerate((ddec_ref[...], udec_ref[...])):
-        arrived(qrecv.at[at], qrecv_sem.at[at])
-        columns = qrecv[at]
-        turned = jnp.transpose(jnp.concatenate([columns, pltpu.roll(columns, n, 1)], axis=0))[:n]
-        out_ref[at] = turned * jnp.concatenate([decay, decay], axis=1)
+    pl.when(jnp.logical_not(is_hub))(hand_over)
     for wait in pending:
         wait()
 

time: 39 us -> 38.8 us (level)
  no operation moved by 1% of the time
where the time goes in v6:
time: 38.8 us; the launch traced here: 38.6 us
  Pallas kernels  37.8 us (97%)
  between operations  0.72 us (2%)
    pallas_call x1, Pallas kernels, sweeps(): pl.pallas_call(functools.partial(kernel, dims), out_shape=jax.ShapeDtypeS...  36.7 us
    pallas_call x1, Pallas kernels, sweeps(): pl.pallas_call(add_terms, out_shape=jax.ShapeDtypeStruct((2, n, width), F...  1.14 us

profile of v6, /device:TPU:1, one launch (start us, length us, event | category | flops | bytes accessed | tf_op | source)
XLA Modules:
  0.0 38.6 jit_solution(4172310223976691817)
XLA Ops:
  0.7 0.0 copy-start
  0.7 0.0 copy-start.1
  0.7 0.0 copy-start.2
  0.7 0.0 copy-start.3
  0.7 36.7 %sweeps.1.coef = f32[2,64,128]{2,1,0:T(8,128)S(1)} custom-call(f32[2,64,1024]{2,1,0:T(8,128)} %bitcast.10, f32[2,64,1024]{2,1,0:T(8,128)} %bitcast.6, f32[2,64,1024]{2,1,0:T(8,128)} %bitcast.12, f32[2,64,1024]{2,1,0:T(8,128)} %bitcast.8, f32[2,64,1024]{2,1,0:T(8,128)} %bitcast.13, f32[1,64]{1,0:T(1,128)} %ddec_hbm.1, f32[1,64]{1,0:T(1,128)} %udec_hbm.1, ...), custom_call_target="tpu_custom_call" | custom-call | tf_op jit(solution)/shard_map/sweeps/pallas_call | solution.py:413
  37.4 0.0 copy-done
  37.4 0.0 copy-done.1
  37.4 0.0 copy-done.2
  37.4 0.0 copy-done.3
  37.4 1.1 %add_terms.1 = f32[2,64,1024]{2,1,0:T(8,128)} custom-call(f32[2,64,1024]{2,1,0:T(8,128)S(1)} %bitcast.7, f32[2,64,1024]{2,1,0:T(8,128)S(1)} %bitcast.9, f32[2,64,1024]{2,1,0:T(8,128)S(1)} %bitcast.11, f32[2,64,128]{2,1,0:T(8,128)S(1)} %sweeps.1.coef, s32[1,64]{1,0:T(1,128)S(1)} %copy-done.3, s32[1]{0:T(128)S(6)} %copy.12.count_ref), custom_call_target="tpu_custom_call" | custom-call | tf_op jit(solution)/shard_map/add_terms/pallas_call | solution.py:463
Async XLA Ops:
  0.7 36.8 %copy-start = (f32[1,2,64,1024]{3,2,1,0:T(8,128)S(1)}, f32[1,2,64,1024]{3,2,1,0:T(8,128)}, u32[]{:S(2)}) copy-start(f32[1,2,64,1024]{3,2,1,0:T(8,128)} %param.12) | copy-start | bytes 1572868
  0.7 36.8 %copy-start.1 = (f32[1,2,64,1024]{3,2,1,0:T(8,128)S(1)}, f32[1,2,64,1024]{3,2,1,0:T(8,128)}, u32[]{:S(2)}) copy-start(f32[1,2,64,1024]{3,2,1,0:T(8,128)} %param.14) | copy-start | bytes 1572868
  0.7 36.8 %copy-start.2 = (f32[1,2,64,1024]{3,2,1,0:T(8,128)S(1)}, f32[1,2,64,1024]{3,2,1,0:T(8,128)}, u32[]{:S(2)}) copy-start(f32[1,2,64,1024]{3,2,1,0:T(8,128)} %param.11) | copy-start | bytes 1572868
  0.7 36.8 %copy-start.3 = (s32[1,64]{1,0:T(1,128)S(1)}, s32[1,64]{1,0:T(1,128)}, u32[]{:S(2)}) copy-start(s32[1,64]{1,0:T(1,128)} %list_ref.1) | copy-start | bytes 772

commit v7 on v6

--- a/solution.py
+++ b/solution.py
@@ -381,7 +381,7 @@
         parts.append(jnp.concatenate([jnp.where(left, value, -value), pltpu.roll(value, n, 1)], axis=0))
     c_h, c_l = halves(jnp.concatenate(parts, axis=1))
     c_all = jnp.concatenate([c_h, c_l], axis=0)
-    step = min(256, width)
+    step = min(512, width)
     copies = []
     for k in range(width // step):
         cols = pl.ds(k * step, step)

time: 38.8 us -> 38.8 us (level)
  no operation moved by 1% of the time
where the time goes in v7:
time: 38.8 us; the launch traced here: 38.6 us
  Pallas kernels  37.9 us (98%)
  between operations  0.72 us (2%)
    pallas_call x1, Pallas kernels, sweeps(): pl.pallas_call(functools.partial(kernel, dims), out_shape=jax.ShapeDtypeS...  36.7 us
    pallas_call x1, Pallas kernels, sweeps(): pl.pallas_call(add_terms, out_shape=jax.ShapeDtypeStruct((2, n, width), F...  1.14 us

profile of v7, /device:TPU:1, one launch (start us, length us, event | category | flops | bytes accessed | tf_op | source)
XLA Modules:
  0.0 38.6 jit_solution(15533659214888854668)
XLA Ops:
  0.7 0.0 copy-start
  0.7 0.0 copy-start.1
  0.7 0.0 copy-start.2
  0.7 0.0 copy-start.3
  0.7 36.7 %sweeps.1.coef = f32[2,64,128]{2,1,0:T(8,128)S(1)} custom-call(f32[2,64,1024]{2,1,0:T(8,128)} %bitcast.10, f32[2,64,1024]{2,1,0:T(8,128)} %bitcast.6, f32[2,64,1024]{2,1,0:T(8,128)} %bitcast.12, f32[2,64,1024]{2,1,0:T(8,128)} %bitcast.8, f32[2,64,1024]{2,1,0:T(8,128)} %bitcast.13, f32[1,64]{1,0:T(1,128)} %ddec_hbm.1, f32[1,64]{1,0:T(1,128)} %udec_hbm.1, ...), custom_call_target="tpu_custom_call" | custom-call | tf_op jit(solution)/shard_map/sweeps/pallas_call | solution.py:413
  37.4 0.0 copy-done
  37.4 0.0 copy-done.1
  37.4 0.0 copy-done.2
  37.4 0.0 copy-done.3
  37.4 1.1 %add_terms.1 = f32[2,64,1024]{2,1,0:T(8,128)} custom-call(f32[2,64,1024]{2,1,0:T(8,128)S(1)} %bitcast.7, f32[2,64,1024]{2,1,0:T(8,128)S(1)} %bitcast.9, f32[2,64,1024]{2,1,0:T(8,128)S(1)} %bitcast.11, f32[2,64,128]{2,1,0:T(8,128)S(1)} %sweeps.1.coef, s32[1,64]{1,0:T(1,128)S(1)} %copy-done.3, s32[1]{0:T(128)S(6)} %copy.12.count_ref), custom_call_target="tpu_custom_call" | custom-call | tf_op jit(solution)/shard_map/add_terms/pallas_call | solution.py:463
Async XLA Ops:
  0.7 36.8 %copy-start = (f32[1,2,64,1024]{3,2,1,0:T(8,128)S(1)}, f32[1,2,64,1024]{3,2,1,0:T(8,128)}, u32[]{:S(2)}) copy-start(f32[1,2,64,1024]{3,2,1,0:T(8,128)} %param.12) | copy-start | bytes 1572868
  0.7 36.8 %copy-start.1 = (f32[1,2,64,1024]{3,2,1,0:T(8,128)S(1)}, f32[1,2,64,1024]{3,2,1,0:T(8,128)}, u32[]{:S(2)}) copy-start(f32[1,2,64,1024]{3,2,1,0:T(8,128)} %param.14) | copy-start | bytes 1572868
  0.7 36.8 %copy-start.2 = (f32[1,2,64,1024]{3,2,1,0:T(8,128)S(1)}, f32[1,2,64,1024]{3,2,1,0:T(8,128)}, u32[]{:S(2)}) copy-start(f32[1,2,64,1024]{3,2,1,0:T(8,128)} %param.11) | copy-start | bytes 1572868
  0.7 36.8 %copy-start.3 = (s32[1,64]{1,0:T(1,128)S(1)}, s32[1,64]{1,0:T(1,128)}, u32[]{:S(2)}) copy-start(s32[1,64]{1,0:T(1,128)} %list_ref.1) | copy-start | bytes 772
